TPU v7x, 32 devices: a whole 2x2x4 slice. The times are simulated.
32 devices in a mesh: row: 8 (over z, x), col: 4 (over y, core), ga: 1.
Axes of the slice: x: 2, y: 2, z: 4, core: 2. Of those that a mesh axis runs over, the one named last changes fastest.
Arguments:
- pair_density: float32 [512, 24, 3072], P('row', None, 'ga'), may hold values from -6 to 6
- coulomb: float32 [3072], P('ga'), may hold values from 0.1 to 2
Outputs:
- kernel: float32 [12288, 12288], P('row', 'col')
All inputs are finite; a program needn't handle non-finite values.
Results may differ from a plain program's by a relative error of at most 0.00011.
Values sent between devices are 32-bit elements; how exact they have to be, the bound alone decides.
A program may use at most 192 MiB of HBM per device.

v0:
```python
import jax
import jax.numpy as jnp
from jax import lax
from jax.sharding import PartitionSpec as P


def contract(left_rows, right_rows):
    return lax.dot_general(
        left_rows,
        right_rows,
        (((1,), (1,)), ((), ())),
        precision=lax.Precision.HIGHEST,
        preferred_element_type=jnp.float32,
    )


def local(pair_density, coulomb):
    row_count = lax.axis_size("row")
    col_count = lax.axis_size("col")
    here_col = lax.axis_index("col")
    doubled = 2.0 * coulomb
    local_k, bands, g_width = pair_density.shape
    grouped = pair_density.reshape(local_k // col_count, col_count, bands, g_width)
    own_columns = lax.dynamic_index_in_dim(grouped, here_col, 1, keepdims=False)
    by_owner = pair_density.reshape(local_k // row_count, row_count, bands, g_width)
    received = lax.all_to_all(by_owner, "row", split_axis=1, concat_axis=0, tiled=True)
    rows_data = received.reshape(local_k, bands, g_width)
    piece = lax.all_gather(own_columns, "row", axis=0, tiled=True)
    weighted = rows_data.reshape(local_k * bands, g_width) * doubled[None, :]
    partial_value = contract(weighted, piece.reshape(piece.shape[0] * bands, g_width))
    summed = lax.psum(partial_value, "ga")
    total_k = local_k * row_count
    return summed / jnp.float32(total_k)


def solution(mesh):
    placed = (P("row", None, "ga"), P("ga"))
    return jax.shard_map(
        local, mesh=mesh, in_specs=placed, out_specs=P("row", "col"), check_vma=False
    )
```

profile of v0, /device:TPU:26, one launch (start us, length us, event | category | flops | bytes accessed | tf_op | source)
XLA Modules:
  0.0 1156.7 jit_solution(15189030200028209390)
XLA Ops:
  6.5 0.0 all-gather.3.cloned.1.call-start
  6.5 5.1 constant_dynamic-slice_fusion
  11.6 0.0 all-gather.3.cloned.1.call-update
  11.6 13.2 %copy.4 = f32[8,8,24,3072]{3,2,0,1:T(8,128)} copy(f32[8,8,24,3072]{3,2,1,0:T(8,128)} %bitcast.11) | data formatting | bytes 37748736 | tf_op jit(solution)/shard_map/reshape | solution.py:25
  24.8 0.0 copy-start
  24.8 6.1 all-to-all-start
  30.9 0.0 copy-done
  30.9 599.0 %all-to-all-done = f32[8,8,24,3072]{3,2,0,1:T(8,128)} async-done(((f32[8,8,24,3072]{3,2,0,1:T(8,128)}), f32[8,8,24,3072]{3,2,0,1:T(8,128)}, u32[]{:S(2)}, u32[]{:S(2)}) %all-to-all-start) | async-done | bytes 18874400 | tf_op jit(solution)/shard_map/all_to_all | solution.py:26
  629.9 13.0 %bitcast_multiply_fusion = f32[8,8,1,24,3072]{4,3,0,1,2:T(8,128)} fusion(f32[8,8,24,3072]{3,2,0,1:T(8,128)} %all-to-all-done, f32[3072]{0:T(1024)S(1)} %broadcast_multiply_fusion), kind=kLoop, calls=%fused_computation | loop fusion | flops 4718592 | bytes 37761024 | tf_op jit(solution)/shard_map/mul | solution.py:29
  642.8 315.6 %all-gather.3.cloned.1.call-done = f32[128,1,24,3072]{3,2,1,0:T(8,128)} async-done(((f32[16,1,24,3072]{3,2,1,0:T(8,128)}), f32[128,1,24,3072]{3,2,1,0:T(8,128)}) %all-gather.3.cloned.1.call-update) | async-done | bytes 37748752 | tf_op jit(solution)/shard_map/all_gather | solution.py:28
  958.5 191.4 %convolution_multiply_fusion = f32[1536,3072]{1,0:T(8,128)} fusion(f32[1536,3072]{1,0:T(8,128)} %bitcast.12, f32[3072,3072]{1,0:T(8,128)} %bitcast.13), kind=kOutput, calls=%fused_computation.1 | convolution fusion | flops 173950894080 | bytes 75497472 | tf_op jit(solution)/shard_map/dot_general | solution.py:8
  (1 shorter events, 0.0 us)
Async XLA Ops:
  6.5 951.9 %all-gather.3.cloned.1.call-start = ((), (), s32[]{:S(2)}) async-start(), calls=%async_computation.1 | async-start | bytes 42467328 | tf_op jit(solution)/shard_map/all_gather | solution.py:28
  24.8 6.1 copy-start
  24.8 605.1 %all-to-all-start = ((f32[8,8,24,3072]{3,2,0,1:T(8,128)}), f32[8,8,24,3072]{3,2,0,1:T(8,128)}, u32[]{:S(2)}, u32[]{:S(2)}) async-start(f32[8,8,24,3072]{3,2,0,1:T(8,128)} %copy.4), calls=%async_computation | async-start | bytes 37748736 | tf_op jit(solution)/shard_map/all_to_all | solution.py:26
Sparse Core Ops, SparseCore 0:
  11.7 946.6 all-gather.2
where the time goes:
time: 1160 us
  waiting for transfers between devices  915 us (79%)
  matrix products  191 us (16%)
  local copies, waits for them, and re-layouts  18.2 us (2%)
  between operations  13.4 us (1%)
  other arithmetic  13 us (1%)
    all_to_all x1, waiting for transfers between devices, local(): lax.all_to_all(by_owner, 'row', split_axis=1, concat_axis=0, tiled=True)  599 us
    all_gather x1, waiting for transfers between devices, local(): piece = lax.all_gather(own_columns, 'row', axis=0, tiled=True)  316 us
    dot_general x1, matrix products, contract(): lax.dot_general(left_rows, right_rows, (((1,), (1,)), ((), ())), precisio...  191 us
  transfers between devices with their start and end apart: 2, of which 2 were waited for; matrix products, arithmetic and copies ran while one was open for 2% of the time, Pallas kernels for 0%

commit v1 on v0

v1 whole, which is shorter than its diff:
```python
import functools

import jax
import jax.numpy as jnp
from jax import lax
from jax.sharding import PartitionSpec as P

LANES = 128
SHARES = (4, 4, 4, 4, 4, 2, 2)


def contract(left_rows, right_rows):
    return lax.dot_general(
        left_rows,
        right_rows,
        (((1,), (1,)), ((), ())),
        precision=lax.Precision.HIGH,
        preferred_element_type=jnp.float32,
    )


def widths_of(total):
    units, shares = total // LANES, sum(SHARES)
    cuts, seen = [0], 0
    for share in SHARES:
        seen += share
        cuts.append(units * seen // shares * LANES)
    cuts[-1] = total
    return [(a, b) for a, b in zip(cuts, cuts[1:]) if b > a]


def spread(rows, row_count, col_count):
    here_row, here_col = lax.axis_index("row"), lax.axis_index("col")
    away = jnp.bitwise_xor(here_col, here_row % col_count)
    bit = col_count // 2
    while bit:
        pairs = []
        for r in range(row_count):
            for c in range(col_count):
                if (c ^ (r % col_count)) % (2 * bit) == 0:
                    pairs.append((r * col_count + c, r * col_count + (c ^ bit)))
        got = lax.ppermute(rows, ("row", "col"), pairs)
        rows = jnp.where(away % (2 * bit) == bit, got, rows)
        bit //= 2
    return rows


def local(pair_density, coulomb):
    row_count = lax.axis_size("row")
    col_count = lax.axis_size("col")
    here_row = lax.axis_index("row")
    here_col = lax.axis_index("col")
    local_k, bands, g_width = pair_density.shape
    total_k = local_k * row_count
    scale = (2.0 * coulomb) / jnp.float32(total_k)
    grouped = pair_density.reshape(local_k // col_count, col_count, bands, g_width)
    ratio = row_count // col_count
    total = None
    for start, stop in widths_of(g_width):
        width = stop - start
        own = lax.dynamic_slice(
            grouped, (0, here_col, 0, start), (local_k // col_count, 1, bands, width)
        )[:, 0]
        piece = lax.all_gather(own, "row", axis=0, tiled=True)
        paired = piece.reshape(piece.shape[0] // ratio, ratio, bands, width)
        rows = lax.dynamic_index_in_dim(paired, here_row // col_count, 1, keepdims=False)
        rows = spread(rows, row_count, col_count)
        weighted = rows.reshape(local_k * bands, width) * scale[None, start:stop]
        part = contract(weighted, piece.reshape(piece.shape[0] * bands, width))
        total = part if total is None else total + part
    return lax.psum(total, "ga")


def solution(mesh):
    placed = (P("row", None, "ga"), P("ga"))
    return jax.shard_map(
        local, mesh=mesh, in_specs=placed, out_specs=P("row", "col"), check_vma=False
    )
```

time: 1160 us -> 853 us (0.74)
  the two profiles are of different devices: /device:TPU:26 before, /device:TPU:7 now
where the time goes in v1:
time: 853 us; the launch traced here: 844 us
  waiting for transfers between devices  571 us (67%)
  matrix products  149 us (17%)
  other arithmetic  45.8 us (5%)
  local copies, waits for them, and re-layouts  32.5 us (4%)
  starting transfers between devices  31.7 us (4%)
  between operations  14.3 us (2%)
    all_gather x7, waiting for transfers between devices, local(): piece = lax.all_gather(own, 'row', axis=0, tiled=True)  568 us
    dot_general x7, matrix products, contract(): lax.dot_general(left_rows, right_rows, (((1,), (1,)), ((), ())), precisio...  149 us
    ppermute x14, starting transfers between devices, spread(): got = lax.ppermute(rows, ('row', 'col'), pairs)  31.5 us
    select_n x7, other arithmetic, spread(): rows = jnp.where(away % (2 * bit) == bit, got, rows)  26.2 us
    squeeze x7, local copies, waits for them, and re-layouts, local(): lax.dynamic_index_in_dim(paired, here_row // col_count, 1, keepdims=False)  25.1 us
    mul x7, other arithmetic, local(): weighted = rows.reshape(local_k * bands, width) * scale[None, start:stop]  19.5 us
  transfers between devices with their start and end apart: 21, of which 7 were waited for; matrix products, arithmetic and copies ran while one was open for 19% of the time, Pallas kernels for 0%

profile of v1, /device:TPU:7, one launch (start us, length us, event | category | flops | bytes accessed | tf_op | source)
XLA Modules:
  0.0 844.3 jit_solution(10733142916336064370)
XLA Ops:
  8.7 4.1 constant_dynamic-slice_fusion.5
  16.1 52.0 %all-gather.25.cloned.1.call-done = f32[128,1,24,256]{3,2,1,0:T(8,128)} async-done(((f32[16,1,24,256]{3,2,1,0:T(8,128)}), f32[128,1,24,256]{3,2,1,0:T(8,128)}) %all-gather.25.cloned.1.call-update) | async-done | bytes 3145744 | tf_op jit(solution)/shard_map/all_gather | solution.py:64
  72.1 96.0 %all-gather.15.cloned.1.call-done = f32[128,1,24,512]{3,2,1,0:T(8,128)} async-done(((f32[16,1,24,512]{3,2,1,0:T(8,128)}), f32[128,1,24,512]{3,2,1,0:T(8,128)}) %all-gather.15.cloned.1.call-update) | async-done | bytes 6291472 | tf_op jit(solution)/shard_map/all_gather | solution.py:64
  168.1 3.9 dynamic-slice_bitcast_fusion.4
  173.3 93.9 %all-gather.17.cloned.1.call-done = f32[128,1,24,512]{3,2,1,0:T(8,128)} async-done(((f32[16,1,24,512]{3,2,1,0:T(8,128)}), f32[128,1,24,512]{3,2,1,0:T(8,128)}) %all-gather.17.cloned.1.call-update) | async-done | bytes 6291472 | tf_op jit(solution)/shard_map/all_gather | solution.py:64
  272.3 54.7 %all-gather.27.cloned.1.call-done = f32[128,1,24,256]{3,2,1,0:T(8,128)} async-done(((f32[16,1,24,256]{3,2,1,0:T(8,128)}), f32[128,1,24,256]{3,2,1,0:T(8,128)}) %all-gather.27.cloned.1.call-update) | async-done | bytes 3145744 | tf_op jit(solution)/shard_map/all_gather | solution.py:64
  331.0 95.9 %all-gather.19.cloned.1.call-done = f32[128,1,24,512]{3,2,1,0:T(8,128)} async-done(((f32[16,1,24,512]{3,2,1,0:T(8,128)}), f32[128,1,24,512]{3,2,1,0:T(8,128)}) %all-gather.19.cloned.1.call-update) | async-done | bytes 6291472 | tf_op jit(solution)/shard_map/all_gather | solution.py:64
  426.8 4.0 dynamic-slice_bitcast_fusion.2
  444.3 81.5 %all-gather.21.cloned.1.call-done = f32[128,1,24,512]{3,2,1,0:T(8,128)} async-done(((f32[16,1,24,512]{3,2,1,0:T(8,128)}), f32[128,1,24,512]{3,2,1,0:T(8,128)}) %all-gather.21.cloned.1.call-update) | async-done | bytes 6291472 | tf_op jit(solution)/shard_map/all_gather | solution.py:64
  525.8 3.9 dynamic-slice_bitcast_fusion.1
  531.0 93.8 %all-gather.23.cloned.1.call-done = f32[128,1,24,512]{3,2,1,0:T(8,128)} async-done(((f32[16,1,24,512]{3,2,1,0:T(8,128)}), f32[128,1,24,512]{3,2,1,0:T(8,128)}) %all-gather.23.cloned.1.call-update) | async-done | bytes 6291472 | tf_op jit(solution)/shard_map/all_gather | solution.py:64
  624.9 4.0 dynamic-slice_bitcast_fusion
  633.9 5.7 collective-permute-start.1
  639.6 4.4 broadcast_select_fusion.3
  656.9 10.8 %fusion.7 = f32[1536,3072]{1,0:T(8,128)} fusion(f32[1536,256]{1,0:T(8,128)S(1)} %bitcast.103, f32[3072,256]{1,0:T(8,128)S(1)} %bitcast.98), kind=kOutput, calls=%fused_computation.37 | convolution fusion | flops 7247757312 | bytes 23592960 | tf_op jit(solution)/shard_map/dot_general | solution.py:13
  667.6 4.3 broadcast_select_fusion.1
  675.0 4.3 broadcast_select_fusion
  684.8 4.6 select_multiply_fusion.3
  693.1 18.2 %fusion.2 = f32[1536,3072]{1,0:T(8,128)} fusion(f32[1536,512]{1,0:T(8,128)S(1)} %bitcast.91, f32[3072,512]{1,0:T(8,128)S(1)} %bitcast.68), kind=kOutput, calls=%fused_computation.32 | convolution fusion | flops 14495514624 | bytes 28311552 | tf_op jit(solution)/shard_map/dot_general | solution.py:13
  711.3 20.8 %fusion.3 = f32[1536,3072]{1,0:T(8,128)} fusion(f32[1536,512]{1,0:T(8,128)} %bitcast.93, f32[3072,512]{1,0:T(8,128)S(1)} %bitcast.75), kind=kOutput, calls=%fused_computation.33 | convolution fusion | flops 14495514624 | bytes 28311552 | tf_op jit(solution)/shard_map/dot_general | solution.py:13
  735.0 18.6 %fusion.4 = f32[1536,3072]{1,0:T(8,128)} fusion(f32[1536,512]{1,0:T(8,128)S(1)} %bitcast.92, f32[3072,512]{1,0:T(8,128)S(1)} %bitcast.80), kind=kOutput, calls=%fused_computation.34 | convolution fusion | flops 14495514624 | bytes 28311552 | tf_op jit(solution)/shard_map/dot_general | solution.py:13
  753.5 18.4 %fusion.5 = f32[1536,3072]{1,0:T(8,128)} fusion(f32[1536,512]{1,0:T(8,128)S(1)} %bitcast.94, f32[3072,512]{1,0:T(8,128)S(1)} %bitcast.90), kind=kOutput, calls=%fused_computation.35 | convolution fusion | flops 14495514624 | bytes 28311552 | tf_op jit(solution)/shard_map/dot_general | solution.py:13
  774.6 18.6 %fusion.6 = f32[1536,3072]{1,0:T(8,128)} fusion(f32[1536,512]{1,0:T(8,128)S(1)} %bitcast.95, f32[3072,512]{1,0:T(8,128)S(1)} %bitcast.85), kind=kOutput, calls=%fused_computation.36 | convolution fusion | flops 14495514624 | bytes 28311552 | tf_op jit(solution)/shard_map/dot_general | solution.py:13
  793.2 43.8 %add_add_fusion = f32[1536,3072]{1,0:T(8,128)} fusion(f32[1536,3072]{1,0:T(8,128)} %fusion.7, f32[1536,3072]{1,0:T(8,128)} %fusion.6, f32[1536,3072]{1,0:T(8,128)} %fusion.5, f32[1536,3072]{1,0:T(8,128)} %fusion.4, f32[1536,3072]{1,0:T(8,128)} %fusion.2, f32[1536,3072]{1,0:T(8,128)} %fusion.3, f32[1536,256]{1,0:T(8,128)} %bitcast.102, ...), kind=kOutput, calls=%fused_computation | convolution fusion | flops 7276068864 | bytes 136839168 | tf_op jit(solution)/shard_map/dot_general | solution.py:13
  (106 shorter events, 69.8 us)
Async XLA Ops:
  6.5 61.5 %all-gather.25.cloned.1.call-start = ((), (), s32[]{:S(2)}) async-start(), calls=%async_computation.5 | async-start | bytes 3538944 | tf_op jit(solution)/shard_map/all_gather | solution.py:64
  8.6 159.4 %all-gather.15.cloned.1.call-start = ((), (), s32[]{:S(2)}) async-start(), calls=%async_computation | async-start | bytes 7077888 | tf_op jit(solution)/shard_map/all_gather | solution.py:64
  12.8 254.3 %all-gather.17.cloned.1.call-start = ((), (), s32[]{:S(2)}) async-start(), calls=%async_computation.1 | async-start | bytes 7077888 | tf_op jit(solution)/shard_map/all_gather | solution.py:64
  13.5 313.5 %all-gather.27.cloned.1.call-start = ((), (), s32[]{:S(2)}) async-start(), calls=%async_computation.6 | async-start | bytes 3538944 | tf_op jit(solution)/shard_map/all_gather | solution.py:64
  14.1 412.7 %all-gather.19.cloned.1.call-start = ((), (), s32[]{:S(2)}) async-start(), calls=%async_computation.2 | async-start | bytes 7077888 | tf_op jit(solution)/shard_map/all_gather | solution.py:64
  14.7 511.1 %all-gather.21.cloned.1.call-start = ((), (), s32[]{:S(2)}) async-start(), calls=%async_computation.3 | async-start | bytes 7077888 | tf_op jit(solution)/shard_map/all_gather | solution.py:64
  15.3 609.6 %all-gather.23.cloned.1.call-start = ((), (), s32[]{:S(2)}) async-start(), calls=%async_computation.4 | async-start | bytes 7077888 | tf_op jit(solution)/shard_map/all_gather | solution.py:64
  70.8 361.6 %collective-permute-start.10 = (f32[64,24,256]{2,1,0:T(8,128)}, f32[64,24,256]{2,1,0:T(8,128)}, u32[]{:S(2)}, u32[]{:S(2)}) collective-permute-start(f32[64,24,256]{2,1,0:T(8,128)} %dynamic-slice_bitcast_fusion.6), channel_id=1, source_target_pairs={{0,2},{5,7},{10,8},{15,13},{16,18},{21,23},{26,24},{31,29}} | collective-permute-start | bytes 4718600 | tf_op jit(solution)/shard_map/ppermute | solution.py:42
  172.0 456.9 %collective-permute-start = (f32[64,24,512]{2,1,0:T(8,128)}, f32[64,24,512]{2,1,0:T(8,128)}, u32[]{:S(2)}, u32[]{:S(2)}) collective-permute-start(f32[64,24,512]{2,1,0:T(8,128)} %dynamic-slice_bitcast_fusion.4), channel_id=1, source_target_pairs={{0,2},{5,7},{10,8},{15,13},{16,18},{21,23},{26,24},{31,29}} | collective-permute-start | bytes 9437192 | tf_op jit(solution)/shard_map/ppermute | solution.py:42
  271.0 362.9 %collective-permute-start.2 = (f32[64,24,512]{2,1,0:T(8,128)}, f32[64,24,512]{2,1,0:T(8,128)}, u32[]{:S(2)}, u32[]{:S(2)}) collective-permute-start(f32[64,24,512]{2,1,0:T(8,128)} %dynamic-slice_bitcast_fusion.3), channel_id=1, source_target_pairs={{0,2},{5,7},{10,8},{15,13},{16,18},{21,23},{26,24},{31,29}} | collective-permute-start | bytes 9437192 | tf_op jit(solution)/shard_map/ppermute | solution.py:42
  329.7 109.2 %collective-permute-start.12 = (f32[64,24,256]{2,1,0:T(8,128)}, f32[64,24,256]{2,1,0:T(8,128)}, u32[]{:S(2)}, u32[]{:S(2)}) collective-permute-start(f32[64,24,256]{2,1,0:T(8,128)} %dynamic-slice_bitcast_fusion.5), channel_id=1, source_target_pairs={{0,2},{5,7},{10,8},{15,13},{16,18},{21,23},{26,24},{31,29}} | collective-permute-start | bytes 4718600 | tf_op jit(solution)/shard_map/ppermute | solution.py:42
  430.9 213.1 %collective-permute-start.4 = (f32[64,24,512]{2,1,0:T(8,128)}, f32[64,24,512]{2,1,0:T(8,128)}, u32[]{:S(2)}, u32[]{:S(2)}) collective-permute-start(f32[64,24,512]{2,1,0:T(8,128)} %dynamic-slice_bitcast_fusion.2), channel_id=1, source_target_pairs={{0,2},{5,7},{10,8},{15,13},{16,18},{21,23},{26,24},{31,29}} | collective-permute-start | bytes 9437192 | tf_op jit(solution)/shard_map/ppermute | solution.py:42
  435.3 94.4 %collective-permute-start.11 = (f32[64,24,256]{2,1,0:T(8,128)}, f32[64,24,256]{2,1,0:T(8,128)S(1)}, u32[]{:S(2)}, u32[]{:S(2)}) collective-permute-start(f32[64,24,256]{2,1,0:T(8,128)} %broadcast_select_fusion.6), channel_id=1, source_target_pairs={{0,1},{2,3},{5,4},{7,6},{8,9},{10,11},{13,12},{15,14},{16,17},{18,... | collective-permute-start | bytes 4718600 | tf_op jit(solution)/shard_map/ppermute | solution.py:42
  441.9 208.9 %collective-permute-start.13 = (f32[64,24,256]{2,1,0:T(8,128)}, f32[64,24,256]{2,1,0:T(8,128)}, u32[]{:S(2)}, u32[]{:S(2)}) collective-permute-start(f32[64,24,256]{2,1,0:T(8,128)} %broadcast_select_fusion.5), channel_id=1, source_target_pairs={{0,1},{2,3},{5,4},{7,6},{8,9},{10,11},{13,12},{15,14},{16,17},{18,... | collective-permute-start | bytes 4718600 | tf_op jit(solution)/shard_map/ppermute | solution.py:42
  529.7 99.2 %copy-start.6 = (f32[64,24,256]{2,1,0:T(8,128)}, f32[64,24,256]{2,1,0:T(8,128)S(1)}, u32[]{:S(2)}) copy-start(f32[64,24,256]{2,1,0:T(8,128)S(1)} %collective-permute-done.11) | copy-start | bytes 4718596
  529.7 137.9 %collective-permute-start.6 = (f32[64,24,512]{2,1,0:T(8,128)}, f32[64,24,512]{2,1,0:T(8,128)}, u32[]{:S(2)}, u32[]{:S(2)}) collective-permute-start(f32[64,24,512]{2,1,0:T(8,128)} %dynamic-slice_bitcast_fusion.1), channel_id=1, source_target_pairs={{0,2},{5,7},{10,8},{15,13},{16,18},{21,23},{26,24},{31,29}} | collective-permute-start | bytes 9437192 | tf_op jit(solution)/shard_map/ppermute | solution.py:42
  628.9 46.1 %collective-permute-start.8 = (f32[64,24,512]{2,1,0:T(8,128)}, f32[64,24,512]{2,1,0:T(8,128)}, u32[]{:S(2)}, u32[]{:S(2)}) collective-permute-start(f32[64,24,512]{2,1,0:T(8,128)} %dynamic-slice_bitcast_fusion), channel_id=1, source_target_pairs={{0,2},{5,7},{10,8},{15,13},{16,18},{21,23},{26,24},{31,29}} | collective-permute-start | bytes 9437192 | tf_op jit(solution)/shard_map/ppermute | solution.py:42
  633.9 48.4 %collective-permute-start.1 = (f32[64,24,512]{2,1,0:T(8,128)S(1)}, f32[64,24,512]{2,1,0:T(8,128)}, u32[]{:S(2)}, u32[]{:S(2)}) collective-permute-start(f32[64,24,512]{2,1,0:T(8,128)S(1)} %broadcast_select_fusion.4), channel_id=1, source_target_pairs={{0,1},{2,3},{5,4},{7,6},{8,9},{10,11},{13,12},{15,14},{16,17},{18,... | collective-permute-start | bytes 9437192 | tf_op jit(solution)/shard_map/ppermute | solution.py:42
  644.0 40.8 %collective-permute-start.3 = (f32[64,24,512]{2,1,0:T(8,128)}, f32[64,24,512]{2,1,0:T(8,128)}, u32[]{:S(2)}, u32[]{:S(2)}) collective-permute-start(f32[64,24,512]{2,1,0:T(8,128)} %broadcast_select_fusion.3), channel_id=1, source_target_pairs={{0,1},{2,3},{5,4},{7,6},{8,9},{10,11},{13,12},{15,14},{16,17},{18,... | collective-permute-start | bytes 9437192 | tf_op jit(solution)/shard_map/ppermute | solution.py:42
  650.8 38.6 %collective-permute-start.5 = (f32[64,24,512]{2,1,0:T(8,128)S(1)}, f32[64,24,512]{2,1,0:T(8,128)S(1)}, u32[]{:S(2)}, u32[]{:S(2)}) collective-permute-start(f32[64,24,512]{2,1,0:T(8,128)S(1)} %broadcast_select_fusion.2), channel_id=1, source_target_pairs={{0,1},{2,3},{5,4},{7,6},{8,9},{10,11},{13,12},{15,14},{16,17},{18,... | collective-permute-start | bytes 9437192 | tf_op jit(solution)/shard_map/ppermute | solution.py:42
  671.9 60.2 %collective-permute-start.7 = (f32[64,24,512]{2,1,0:T(8,128)}, f32[64,24,512]{2,1,0:T(8,128)}, u32[]{:S(2)}, u32[]{:S(2)}) collective-permute-start(f32[64,24,512]{2,1,0:T(8,128)} %broadcast_select_fusion.1), channel_id=1, source_target_pairs={{0,1},{2,3},{5,4},{7,6},{8,9},{10,11},{13,12},{15,14},{16,17},{18,... | collective-permute-start | bytes 9437192 | tf_op jit(solution)/shard_map/ppermute | solution.py:42
  679.4 92.6 %collective-permute-start.9 = (f32[64,24,512]{2,1,0:T(8,128)}, f32[64,24,512]{2,1,0:T(8,128)}, u32[]{:S(2)}, u32[]{:S(2)}) collective-permute-start(f32[64,24,512]{2,1,0:T(8,128)} %broadcast_select_fusion), channel_id=1, source_target_pairs={{0,1},{2,3},{5,4},{7,6},{8,9},{10,11},{13,12},{15,14},{16,17},{18,... | collective-permute-start | bytes 9437192 | tf_op jit(solution)/shard_map/ppermute | solution.py:42
  693.1 41.9 %slice-start.6 = ((s8[6291456]{0:T(1024)(128)(4,1)}), s8[4194304]{0:T(1024)(128)(4,1)S(1)}, s32[]{:S(2)}) async-start(s8[6291456]{0:T(1024)(128)(4,1)} %bitcast.78), calls=%async_computation.13 | async-start | bytes 8388608
  711.3 23.7 %slice-start.7 = ((s8[6291456]{0:T(1024)(128)(4,1)}), s8[2097152]{0:T(1024)(128)(4,1)S(1)}, s32[]{:S(2)}) async-start(s8[6291456]{0:T(1024)(128)(4,1)} %bitcast.78), calls=%async_computation.14 | async-start | bytes 4194304
  (18 other events, 192.3 us)
Sparse Core Ops, SparseCore 0:
  9.5 58.4 all-gather.24
  70.2 97.7 all-gather.14
  170.2 96.8 all-gather.16
  269.2 57.7 all-gather.26
  329.0 97.7 all-gather.18
  428.9 96.8 all-gather.20
  528.0 96.8 all-gather.22
